TPU v7x, 128 devices: a whole 4x4x4 slice. The times are simulated.
128 devices in a mesh: rep: 16 (over y, x_hi, core), fsdp: 8 (over x_lo, z).
Axes of the slice: x: 4 (x_hi: 2, x_lo: 2; x = x_hi * 2 + x_lo), y: 4, z: 4, core: 2. Of those that a mesh axis runs over, the one named last changes fastest.
Arguments:
- replica_inner_weight: bfloat16 [16, 1024, 16384], P('rep', 'fsdp'), may hold values from -30 to 30
- outer_weights: float32 [1024, 16384], P('fsdp'), may hold values from -6 to 6
- momentum: float32 [1024, 16384], P('fsdp', 'rep'), may hold values from -4 to 4
- exponents: int32 [16, 1024, 128], P('rep', 'fsdp'), may hold values from 0 to 2
- levels: int32 [16], replicated, may hold values from -60 to 60, as said below
Outputs:
- inner_next: bfloat16 [16, 1024, 16384], P('rep', 'fsdp')
- momentum_next: float32 [1024, 16384], P('fsdp', 'rep')
- outer_next: float32 [1024, 16384], P('fsdp', 'rep')
Inputs may be any that keep to these rules, and one draw needn't show every extreme that they name: `levels`: 16 distinct values, half of them negative and half positive, ascending.
All inputs are finite; a program needn't handle non-finite values. Where the computation divides by a largest or mean magnitude, that divisor is 1e-20 or more.
Results may differ from a plain program's by a relative error of at most 0.0085.
Values may be sent and summed in bfloat16 or wider, within the bound.
No kernel may reach another device: no remote copies, remote signals or barrier semaphores. Data moves between devices by JAX's collectives and lax.ppermute only.
A program may use at most 128 MiB of HBM per device.

v0:
```python
import jax
import jax.numpy as jnp
from jax import lax
from jax.sharding import Mesh
from jax.sharding import PartitionSpec as P

NLEV = 16
REP = ("rep_0", "rep_1", "rep_2")
FSDP = ("fsdp_0", "fsdp_1")
REP_FSDP = ("rep_0", "rep_1", "rep_2", "fsdp_0", "fsdp_1")
softness_factor = 0.02
clip_rms = 0.1
outer_rate = 0.7
outer_mu = 0.9
mix_rate = 0.5


def by_axis(array, axes):
    for axis in axes:
        array = lax.psum(array, axis)
    return array


def encode_grad(pseudo_grad, exponents, levels):
    quantize_grid_points = levels.astype(jnp.float32) / jnp.max(jnp.abs(levels)).astype(jnp.float32)
    block_scale = jnp.exp2(exponents.astype(jnp.float32))[..., None]
    row_count = pseudo_grad.shape[0]
    rescaled_gradient = pseudo_grad.reshape(row_count, exponents.shape[-1], -1) / block_scale
    closest_grid_level = (rescaled_gradient - quantize_grid_points[0]) ** 2
    for grid_level_index in range(1, NLEV):
        closest_grid_level = jnp.minimum(
            closest_grid_level, (rescaled_gradient - quantize_grid_points[grid_level_index]) ** 2
        )
    weighted = jnp.zeros_like(rescaled_gradient)
    weights_sum = jnp.zeros_like(rescaled_gradient)
    for grid_level_index in range(NLEV):
        current_weight = jnp.exp(
            -(
                (rescaled_gradient - quantize_grid_points[grid_level_index]) ** 2
                - closest_grid_level
            )
            / softness_factor
        )
        weighted = weighted + current_weight * quantize_grid_points[grid_level_index]
        weights_sum = weights_sum + current_weight
    coded = block_scale * weighted / weights_sum
    return coded.reshape(row_count, -1).astype(jnp.bfloat16)


def clip_factor(squares, entries):
    return jnp.minimum(
        jnp.float32(1.0), clip_rms / jnp.sqrt(squares / jnp.float32(entries) + 1e-06)
    )


def per_device(replica_inner_weight, outer_weights, momentum, exponents, levels):
    replicas = lax.axis_size(REP)
    row_count, columns = outer_weights.shape
    entries = row_count * lax.axis_size(FSDP) * columns
    width = momentum.shape[1]
    start = lax.axis_index(REP) * width
    coded = encode_grad(
        outer_weights - replica_inner_weight[0].astype(jnp.float32), exponents[0], levels
    )
    share = lax.psum_scatter(coded, REP, scatter_dimension=1, tiled=True).astype(jnp.float32)
    mean_grad = share / jnp.float32(replicas)
    squares = by_axis(jnp.sum(mean_grad * mean_grad), REP_FSDP)
    grad = clip_factor(squares, entries) * mean_grad
    momentum_next = outer_mu * momentum + grad
    outer_piece = lax.dynamic_slice_in_dim(outer_weights, start, width, 1)
    outer_next = outer_piece - outer_rate * (grad + outer_mu * momentum_next)
    outer_half = lax.all_gather(outer_next.astype(jnp.bfloat16), REP, axis=1, tiled=True)
    mixed = mix_rate * outer_half.astype(jnp.float32) + (1.0 - mix_rate) * replica_inner_weight[
        0
    ].astype(jnp.float32)
    inner_next = mixed.astype(jnp.bfloat16)[None]
    return (inner_next, momentum_next, outer_next)


def solution(mesh):
    torus = Mesh(
        mesh.devices.reshape(4, 2, 2, 2, 4), ("rep_0", "rep_1", "rep_2", "fsdp_0", "fsdp_1")
    )
    placed = (P(REP, FSDP, None), P(FSDP, None), P(FSDP, REP), P(REP, FSDP, None), P())
    return jax.shard_map(
        per_device,
        mesh=torus,
        in_specs=placed,
        out_specs=(P(REP, FSDP, None), P(FSDP, REP), P(FSDP, REP)),
        check_vma=False,
    )
```

profile of v0, /device:TPU:1, one launch (start us, length us, event | category | flops | bytes accessed | tf_op | source)
XLA Modules:
  0.0 264.6 jit_solution(7247658938995126674)
XLA Ops:
  7.2 0.0 reduce-scatter.2.cloned.1.call-start
  7.2 1.3 abs_reduce_fusion
  9.2 0.0 copy-start
  9.2 0.8 convert_divide_fusion
  10.0 0.7 fusion.15
  10.7 0.9 exponential_bitcast_fusion
  11.6 2.3 mul.130
  13.9 0.0 copy-done
  13.9 0.0 copy-start.1
  13.9 60.4 %fusion.4 = bf16[128,16384]{1,0:T(8,128)(2,1)} fusion(f32[128,16384]{1,0:T(8,128)} %param.6, f32[16,8,128,128]{3,2,1,0:T(8,128)S(1)} %bitcast.34, bf16[1,128,16384]{2,1,0:T(8,128)(2,1)S(1)} %copy-done, f32[]{:T(128)} %bitcast.17, f32[]{:T(128)} %bitcast.16, f32[]{:T(128)} %bitcast.15, f32[]{:T(128)} %bitcast.14, f32[]{:T(128)} %bitcast.13, f32[]{:T(128)} %bitcast.12, ...), kind=kLoop, calls=%fused_computation.7 | loop fusion | flops 308281344 | bytes 25165888 | tf_op jit(solution)/shard_map/convert_element_type | solution.py:47
  74.3 0.0 reduce-scatter.2.cloned.1.call-update
  74.3 0.0 all-gather.2.cloned.1.call-start
  74.4 82.5 %reduce-scatter.2.cloned.1.call-done = bf16[128,1024]{1,0:T(8,128)(2,1)} async-done(((bf16[128,16384]{1,0:T(8,128)(2,1)}), bf16[128,1024]{1,0:T(8,128)(2,1)}) %reduce-scatter.2.cloned.1.call-update) | async-done | bytes 262160 | tf_op jit(solution)/shard_map/reduce_scatter | solution.py:65
  156.9 1.7 fusion.11
  158.5 8.7 %psum.35 = f32[]{:T(128)} all-reduce(f32[]{:T(128)} %fusion.11), channel_id=1, replica_groups=mesh['rep_0'=4,'rep_1'=2,'rep_2'=2,'fsdp_0'=2,'fsdp_1'=4] {'rep_0'}, use_global_device_ids=true, to_apply=%region_3.0 | all-reduce | flops 1 | bytes 8 | tf_op jit(solution)/shard_map/psum | solution.py:20
  167.3 5.9 %psum.36 = f32[]{:T(128)} all-reduce(f32[]{:T(128)} %psum.35), channel_id=1, replica_groups=mesh['rep_0'=4,'rep_1'=2,'rep_2'=2,'fsdp_0'=2,'fsdp_1'=4] {'rep_1'}, use_global_device_ids=true, to_apply=%region_4.0 | all-reduce | flops 1 | bytes 8 | tf_op jit(solution)/shard_map/psum | solution.py:20
  173.2 7.9 %psum.37 = f32[]{:T(128)} all-reduce(f32[]{:T(128)} %psum.36), channel_id=1, replica_groups=mesh['rep_0'=4,'rep_1'=2,'rep_2'=2,'fsdp_0'=2,'fsdp_1'=4] {'rep_2'}, use_global_device_ids=true, to_apply=%region_5.0 | all-reduce | flops 1 | bytes 8 | tf_op jit(solution)/shard_map/psum | solution.py:20
  181.1 4.4 %psum.38 = f32[]{:T(128)} all-reduce(f32[]{:T(128)} %psum.37), channel_id=1, replica_groups=mesh['rep_0'=4,'rep_1'=2,'rep_2'=2,'fsdp_0'=2,'fsdp_1'=4] {'fsdp_0'}, use_global_device_ids=true, to_apply=%region_6.0 | all-reduce | flops 1 | bytes 8 | tf_op jit(solution)/shard_map/psum | solution.py:20
  185.5 9.3 %psum.39 = f32[]{:T(128)} all-reduce(f32[]{:T(128)} %psum.38), channel_id=1, replica_groups=mesh['rep_0'=4,'rep_1'=2,'rep_2'=2,'fsdp_0'=2,'fsdp_1'=4] {'fsdp_1'}, use_global_device_ids=true, to_apply=%region_7.0 | all-reduce | flops 1 | bytes 8 | tf_op jit(solution)/shard_map/psum | solution.py:20
  195.4 0.0 copy-done.1
  195.4 2.3 fusion.12
  197.8 0.0 all-gather.2.cloned.1.call-update
  197.8 53.3 %all-gather.2.cloned.1.call-done = bf16[128,16384]{1,0:T(8,128)(2,1)} async-done(((bf16[128,1024]{1,0:T(8,128)(2,1)}), bf16[128,16384]{1,0:T(8,128)(2,1)}) %all-gather.2.cloned.1.call-update) | async-done | bytes 4194320 | tf_op jit(solution)/shard_map/all_gather | solution.py:72
  251.1 6.7 %fusion.5 = bf16[1,128,16384]{2,1,0:T(8,128)(2,1)} fusion(bf16[128,16384]{1,0:T(8,128)(2,1)} %all-gather.2.cloned.1.call-done, bf16[1,128,16384]{2,1,0:T(8,128)(2,1)} %param.5), kind=kLoop, calls=%fused_computation.8 | loop fusion | flops 10485760 | bytes 12582912 | tf_op jit(solution)/shard_map/broadcast_in_dim | solution.py:76
Async XLA Ops:
  7.2 149.7 %reduce-scatter.2.cloned.1.call-start = ((), (), s32[]{:S(2)}) async-start(), calls=%async_computation.1 | async-start | bytes 4456448 | tf_op jit(solution)/shard_map/reduce_scatter | solution.py:65
  9.2 4.7 %copy-start = (bf16[1,128,16384]{2,1,0:T(8,128)(2,1)S(1)}, bf16[1,128,16384]{2,1,0:T(8,128)(2,1)}, u32[]{:S(2)}) copy-start(bf16[1,128,16384]{2,1,0:T(8,128)(2,1)} %param.5) | copy-start | bytes 12582916
  13.9 181.5 %copy-start.1 = (f32[128,1024]{1,0:T(8,128)S(1)}, f32[128,1024]{1,0:T(8,128)}, u32[]{:S(2)}) copy-start(f32[128,1024]{1,0:T(8,128)} %param.7) | copy-start | bytes 1572868
  74.3 176.8 %all-gather.2.cloned.1.call-start = ((), (), s32[]{:S(2)}) async-start(), calls=%async_computation.2 | async-start | bytes 4456448 | tf_op jit(solution)/shard_map/all_gather | solution.py:72
Sparse Core Ops, SparseCore 0:
  74.4 82.3 reduce-scatter.1
  197.9 53.0 all-gather.1
where the time goes:
time: 265 us
  waiting for transfers between devices  136 us (51%)
  other arithmetic  74.1 us (28%)
  blocking collectives  36.2 us (14%)
  between operations  15.4 us (6%)
  local copies, waits for them, and re-layouts  3.03 us (1%)
    reduce_scatter x1, waiting for transfers between devices, per_device(): lax.psum_scatter(coded, REP, scatter_dimension=1, tiled=True)  82.5 us
    convert_element_type x1, other arithmetic, encode_grad(): return coded.reshape(row_count, -1).astype(jnp.bfloat16)  60.4 us
    all_gather x1, waiting for transfers between devices, per_device(): lax.all_gather(outer_next.astype(jnp.bfloat16), REP, axis=1, tiled=True)  53.3 us
    psum x5, blocking collectives, by_axis(): array = lax.psum(array, axis)  36.2 us
    broadcast_in_dim x1, other arithmetic, per_device(): inner_next = mixed.astype(jnp.bfloat16)[None]  6.7 us
  transfers between devices with their start and end apart: 2, of which 2 were waited for; matrix products, arithmetic and copies ran while one was open for 0% of the time, Pallas kernels for 0%

commit v1 on v0

--- a/solution.py
+++ b/solution.py
@@ -69,7 +69,12 @@
     momentum_next = outer_mu * momentum + grad
     outer_piece = lax.dynamic_slice_in_dim(outer_weights, start, width, 1)
     outer_next = outer_piece - outer_rate * (grad + outer_mu * momentum_next)
-    outer_half = lax.all_gather(outer_next.astype(jnp.bfloat16), REP, axis=1, tiled=True)
+    outer_half = jnp.concatenate(
+        lax.all_to_all(
+            jnp.stack([outer_next.astype(jnp.bfloat16)] * lax.axis_size(REP)), REP, 0, 0
+        ),
+        axis=1,
+    )
     mixed = mix_rate * outer_half.astype(jnp.float32) + (1.0 - mix_rate) * replica_inner_weight[
         0
     ].astype(jnp.float32)

time: 265 us -> 295 us (1.11)
  local copies, waits for them, and re-layouts: 3.03 us -> 34 us
  starting transfers between devices: 0.08 us -> 7.81 us
  other arithmetic: 74.1 us -> 69.1 us
  waiting for transfers between devices: 136 us -> 132 us
    all_gather x1 -> x0, waiting for transfers between devices: 53.3 us -> none  [per_device(): lax.all_gather(outer_next.astype(jnp.bfloat16), REP, axis=1, tiled=True)]
    all_to_all x0 -> x1, waiting for transfers between devices: none -> 49 us  [per_device(): lax.all_to_all(jnp.stack([outer_next.astype(jnp.bfloat16)] * lax.axis_siz...]
    unnamed x4 -> x10, local copies, waits for them, and re-layouts: 0.01 us -> 24.2 us
    all_to_all x0 -> x1, starting transfers between devices: none -> 7.78 us  [per_device(): lax.all_to_all(jnp.stack([outer_next.astype(jnp.bfloat16)] * lax.axis_siz...]
    broadcast_in_dim x1 -> x0, other arithmetic: 6.7 us -> none  [per_device(): inner_next = mixed.astype(jnp.bfloat16)[None]]
    all_to_all x0 -> x1, local copies, waits for them, and re-layouts: none -> 6.4 us  [per_device(): lax.all_to_all(jnp.stack([outer_next.astype(jnp.bfloat16)] * lax.axis_siz...]
    convert_element_type x0 -> x2, other arithmetic: none -> 5.64 us  [the longest x1 3.18 us: per_device(): outer_half.astype(jnp.float32)]
  transfers between devices with their start and end apart: 2 -> 2, of which waited for: 2 -> 2; matrix products, arithmetic and copies ran while one was open for 0% -> 1% of each run, Pallas kernels for 0% -> 0%
where the time goes in v1:
time: 295 us; the launch traced here: 294 us
  waiting for transfers between devices  132 us (45%)
  other arithmetic  69.1 us (23%)
  blocking collectives  36.2 us (12%)
  local copies, waits for them, and re-layouts  34 us (12%)
  between operations  15.4 us (5%)
  starting transfers between devices  7.81 us (3%)
    reduce_scatter x1, waiting for transfers between devices, per_device(): lax.psum_scatter(coded, REP, scatter_dimension=1, tiled=True)  82.6 us
    convert_element_type x1, other arithmetic, encode_grad(): return coded.reshape(row_count, -1).astype(jnp.bfloat16)  57.6 us
    all_to_all x1, waiting for transfers between devices, per_device(): lax.all_to_all(jnp.stack([outer_next.astype(jnp.bfloat16)] * lax.axis_siz...  49 us
    psum x5, blocking collectives, by_axis(): array = lax.psum(array, axis)  36.2 us
    unnamed x10, local copies, waits for them, and re-layouts  24.2 us
    all_to_all x1, starting transfers between devices, per_device(): lax.all_to_all(jnp.stack([outer_next.astype(jnp.bfloat16)] * lax.axis_siz...  7.78 us
    all_to_all x1, local copies, waits for them, and re-layouts, per_device(): lax.all_to_all(jnp.stack([outer_next.astype(jnp.bfloat16)] * lax.axis_siz...  6.4 us
  transfers between devices with their start and end apart: 2, of which 2 were waited for; matrix products, arithmetic and copies ran while one was open for 1% of the time, Pallas kernels for 0%

profile of v1, /device:TPU:1, one launch (start us, length us, event | category | flops | bytes accessed | tf_op | source)
XLA Modules:
  0.0 294.1 jit_solution(3181373066065009256)
XLA Ops:
  7.2 0.0 reduce-scatter.2.cloned.1.call-start
  7.2 1.3 abs_reduce_fusion
  9.2 0.7 convert_divide_fusion
  9.8 0.7 fusion.13
  10.5 0.9 exponential_bitcast_fusion
  11.4 0.1 copy.9
  11.5 6.4 %copy.10 = bf16[1,128,16384]{1,2,0:T(8,128)(2,1)} copy(bf16[1,128,16384]{2,1,0:T(8,128)(2,1)} %param.5) | data formatting | bytes 8388608 | tf_op args[0]
  17.8 9.0 %copy.8 = f32[128,16384]{0,1:T(8,128)} copy(f32[128,16384]{1,0:T(8,128)} %param.6) | data formatting | bytes 16777216 | tf_op args[1]
  26.8 0.0 copy-start.1
  26.8 57.6 %fusion.4 = bf16[128,16384]{0,1:T(8,128)(2,1)} fusion(f32[128,16384]{0,1:T(8,128)} %copy.8, bf16[1,128,16384]{1,2,0:T(8,128)(2,1)} %copy.10, f32[]{:T(128)} %bitcast.18, f32[]{:T(128)} %bitcast.17, f32[]{:T(128)} %bitcast.16, f32[]{:T(128)} %bitcast.15, f32[]{:T(128)} %bitcast.14, f32[]{:T(128)} %bitcast.13, f32[]{:T(128)} %bitcast.12, f32[]{:T(128)} %bitcast.11, ...), kind=kLoop, calls=%fused_computation.8 | loop fusion | flops 308281344 | bytes 16842816 | tf_op jit(solution)/shard_map/convert_element_type | solution.py:47
  84.5 0.0 reduce-scatter.2.cloned.1.call-update
  84.5 82.6 %reduce-scatter.2.cloned.1.call-done = bf16[128,1024]{0,1:T(8,128)(2,1)} async-done(((bf16[128,16384]{0,1:T(8,128)(2,1)}), bf16[128,1024]{0,1:T(8,128)(2,1)}) %reduce-scatter.2.cloned.1.call-update) | async-done | bytes 262160 | tf_op jit(solution)/shard_map/reduce_scatter | solution.py:65
  167.1 1.7 fusion.10
  168.8 8.7 %psum.35 = f32[]{:T(128)} all-reduce(f32[]{:T(128)} %fusion.10), channel_id=1, replica_groups=mesh['rep_0'=4,'rep_1'=2,'rep_2'=2,'fsdp_0'=2,'fsdp_1'=4] {'rep_0'}, use_global_device_ids=true, to_apply=%region_3.0 | all-reduce | flops 1 | bytes 8 | tf_op jit(solution)/shard_map/psum | solution.py:20
  177.5 5.9 %psum.36 = f32[]{:T(128)} all-reduce(f32[]{:T(128)} %psum.35), channel_id=1, replica_groups=mesh['rep_0'=4,'rep_1'=2,'rep_2'=2,'fsdp_0'=2,'fsdp_1'=4] {'rep_1'}, use_global_device_ids=true, to_apply=%region_4.0 | all-reduce | flops 1 | bytes 8 | tf_op jit(solution)/shard_map/psum | solution.py:20
  183.4 7.9 %psum.37 = f32[]{:T(128)} all-reduce(f32[]{:T(128)} %psum.36), channel_id=1, replica_groups=mesh['rep_0'=4,'rep_1'=2,'rep_2'=2,'fsdp_0'=2,'fsdp_1'=4] {'rep_2'}, use_global_device_ids=true, to_apply=%region_5.0 | all-reduce | flops 1 | bytes 8 | tf_op jit(solution)/shard_map/psum | solution.py:20
  191.3 0.0 copy-done.1
  191.3 0.2 copy.12
  191.5 4.4 %psum.38 = f32[]{:T(128)} all-reduce(f32[]{:T(128)} %psum.37), channel_id=1, replica_groups=mesh['rep_0'=4,'rep_1'=2,'rep_2'=2,'fsdp_0'=2,'fsdp_1'=4] {'fsdp_0'}, use_global_device_ids=true, to_apply=%region_6.0 | all-reduce | flops 1 | bytes 8 | tf_op jit(solution)/shard_map/psum | solution.py:20
  195.9 9.3 %psum.39 = f32[]{:T(128)} all-reduce(f32[]{:T(128)} %psum.38), channel_id=1, replica_groups=mesh['rep_0'=4,'rep_1'=2,'rep_2'=2,'fsdp_0'=2,'fsdp_1'=4] {'fsdp_1'}, use_global_device_ids=true, to_apply=%region_7.0 | all-reduce | flops 1 | bytes 8 | tf_op jit(solution)/shard_map/psum | solution.py:20
  205.9 1.3 fusion.11
  207.2 0.1 copy.13
  207.3 2.5 stack.2
  209.8 7.8 %all-to-all-start = ((bf16[16,128,1024]{2,1,0:T(8,128)(2,1)}), bf16[16,128,1024]{2,1,0:T(8,128)(2,1)}, u32[]{:S(2)}, u32[]{:S(2)}) async-start(bf16[16,128,1024]{2,1,0:T(8,128)(2,1)} %stack.2), calls=%async_computation.1 | async-start | bytes 8388608 | tf_op jit(solution)/shard_map/all_to_all | solution.py:73
  217.6 1.0 copy.17
  218.6 1.0 copy.16
  219.6 49.0 %all-to-all-done = bf16[16,128,1024]{2,1,0:T(8,128)(2,1)} async-done(((bf16[16,128,1024]{2,1,0:T(8,128)(2,1)}), bf16[16,128,1024]{2,1,0:T(8,128)(2,1)}, u32[]{:S(2)}, u32[]{:S(2)}) %all-to-all-start) | async-done | bytes 4194336 | tf_op jit(solution)/shard_map/all_to_all | solution.py:73
  268.6 6.4 %copy.14 = bf16[16,128,1024]{1,2,0:T(8,128)(2,1)} copy(bf16[16,128,1024]{2,1,0:T(8,128)(2,1)} %all-to-all-done) | data formatting | bytes 8388608 | tf_op jit(solution)/shard_map/all_to_all | solution.py:73
  275.0 0.0 copy-start
  275.0 3.2 %convert_element_type.68 = f32[16,128,1024]{1,2,0:T(8,128)S(1)} convert(bf16[16,128,1024]{1,2,0:T(8,128)(2,1)} %copy.14) | non-fusion elementwise | flops 2097152 | bytes 12582912 | tf_op jit(solution)/shard_map/convert_element_type | solution.py:78
  278.2 0.3 copy-done
  278.5 2.5 fusion.2
  280.9 6.4 %copy.15 = bf16[1,128,16384]{2,1,0:T(8,128)(2,1)} copy(bf16[1,128,16384]{1,2,0:T(8,128)(2,1)} %fusion.2) | data formatting | bytes 8388608
Async XLA Ops:
  7.2 159.9 %reduce-scatter.2.cloned.1.call-start = ((), (), s32[]{:S(2)}) async-start(), calls=%async_computation.2 | async-start | bytes 4456448 | tf_op jit(solution)/shard_map/reduce_scatter | solution.py:65
  26.8 164.4 %copy-start.1 = (f32[128,1024]{1,0:T(8,128)S(1)}, f32[128,1024]{1,0:T(8,128)}, u32[]{:S(2)}) copy-start(f32[128,1024]{1,0:T(8,128)} %param.7) | copy-start | bytes 1572868
  209.8 58.8 %all-to-all-start = ((bf16[16,128,1024]{2,1,0:T(8,128)(2,1)}), bf16[16,128,1024]{2,1,0:T(8,128)(2,1)}, u32[]{:S(2)}, u32[]{:S(2)}) async-start(bf16[16,128,1024]{2,1,0:T(8,128)(2,1)} %stack.2), calls=%async_computation.1 | async-start | bytes 8388608 | tf_op jit(solution)/shard_map/all_to_all | solution.py:73
  275.0 3.4 %copy-start = (bf16[1,128,16384]{1,2,0:T(8,128)(2,1)S(1)}, bf16[1,128,16384]{1,2,0:T(8,128)(2,1)}, u32[]{:S(2)}) copy-start(bf16[1,128,16384]{1,2,0:T(8,128)(2,1)} %copy.10) | copy-start | bytes 12582916
Sparse Core Ops, SparseCore 0:
  84.6 82.4 reduce-scatter.1
